TPU v7x, 128 devices: a whole 4x4x4 slice. The times are simulated.
128 devices in a mesh: dp: 32 (over x, z, core), tensor: 4 (over y).
Axes of the slice: x: 4, y: 4, z: 4, core: 2. Of those that a mesh axis runs over, the one named last changes fastest.
Arguments:
- tokens: bfloat16 [16384, 4096], P(('dp', 'tensor')), may hold values from -6 to 6
- norm_gain: float32 [4096], replicated, may hold values from 0.1 to 1.9
- w_query: bfloat16 [4096, 2048], P(None, 'tensor'), may hold values from -2 to 2
- key_weight: bfloat16 [4096, 512], P(None, 'tensor'), may hold values from -0.09375 to 0.09375
- value_weight: bfloat16 [4096, 512], P(None, 'tensor'), may hold values from -0.09375 to 0.09375
- w_out: bfloat16 [2048, 4096], P('tensor'), may hold values from -0.125 to 0.125
- lengths: int32 [16], replicated, may hold values from 1 to 8704, 16384 in all
Outputs:
- layer_out: bfloat16 [16384, 4096], P(('dp', 'tensor'))
Inputs may be any that keep to these rules, and one draw needn't show every extreme that they name: The lengths sum to 16384, and some document has exactly 8704 tokens.
All inputs are finite; a program needn't handle non-finite values.
Results may differ from a plain program's by a relative error of at most 0.0095.
The roundings to bfloat16 on the way count: a program that leaves them out, or rounds other values in their place, can miss the bound.
Values may be sent and summed in bfloat16 or wider, within the bound.
No kernel may reach another device: no remote copies, remote signals or barrier semaphores. Data moves between devices by JAX's collectives and lax.ppermute only.
A program may use at most 128 MiB of HBM per device.

v0:
```python
import jax
import jax.numpy as jnp
from jax import lax
from jax.sharding import PartitionSpec as P

HEAD_SIZE = 128
epsilon = 1e-05
rope_base = 500000.0
masked = -1e30
initial_peak = -1e29


def in_one_piece(arrays, axis, dim, along):
    ends, at = ([], 0)
    for a in arrays[:-1]:
        at += a.shape[along]
        ends.append(at)
    both = jnp.concatenate(arrays, axis=along)
    return tuple(jnp.split(lax.all_gather(both, axis, axis=dim, tiled=True), ends, axis=along))


def doc_starts(lengths, positions):
    doc_ends = jnp.cumsum(lengths)
    closed = (doc_ends[None, :] <= positions[:, None]).astype(jnp.int32)
    return jnp.sum(closed * lengths[None, :], axis=1)


def rotate(vectors, offsets):
    half_width = vectors.shape[-1] // 2
    exponent = jnp.arange(half_width, dtype=jnp.float32) * (-2.0 / vectors.shape[-1])
    frequency = rope_base**exponent
    angles = offsets.astype(jnp.float32)[:, None] * frequency[None, :]
    cos_part = jnp.cos(angles)[:, None, :]
    sin_part = jnp.sin(angles)[:, None, :]
    leading = vectors[..., :half_width]
    trailing = vectors[..., half_width:]
    return jnp.concatenate(
        [leading * cos_part - trailing * sin_part, trailing * cos_part + leading * sin_part],
        axis=-1,
    )


def project(tokens, norm_gain, w_query, key_weight, value_weight, positions, starts):
    count = tokens.shape[0]
    wide = tokens.astype(jnp.float32)
    inverse = lax.rsqrt(jnp.mean(wide * wide, axis=1, keepdims=True) + epsilon)
    normed = (wide * inverse * norm_gain[None, :]).astype(jnp.bfloat16)
    offsets = positions - starts
    query_rows = jnp.dot(normed, w_query, preferred_element_type=jnp.float32).reshape(
        count, -1, HEAD_SIZE
    )
    query_rows = rotate(query_rows, offsets).astype(jnp.bfloat16)
    key = jnp.dot(normed, key_weight, preferred_element_type=jnp.float32).reshape(
        count, -1, HEAD_SIZE
    )
    key = rotate(key, offsets).astype(jnp.bfloat16)
    value_rows = jnp.dot(normed, value_weight, preferred_element_type=jnp.float32).astype(
        jnp.bfloat16
    )
    return (query_rows, key.reshape(count, -1), value_rows)


def attend_block(carry, keys, values, first_key, context):
    query_rows, positions, starts = context
    length = keys.shape[0]
    heads = query_rows.shape[1]
    key_pos = first_key + jnp.arange(length, dtype=jnp.int32)
    useful = (first_key + length - 1 >= starts[0]) & (first_key <= positions[-1])
    scale = query_rows.shape[-1] ** (-0.5)

    def compute(state):
        peak, mass, summed = state
        key_view = keys.reshape(length, heads, -1)
        value_view = values.reshape(length, heads, -1)
        scores = (
            jnp.einsum("qkgd,skd->qkgs", query_rows, key_view, preferred_element_type=jnp.float32)
            * scale
        )
        visible = (key_pos[None, :] >= starts[:, None]) & (key_pos[None, :] <= positions[:, None])
        scores = jnp.where(visible[:, None, None, :], scores, masked)
        fresh = jnp.maximum(peak, jnp.max(scores, axis=-1))
        shrink = jnp.exp(peak - fresh)
        probs = jnp.exp(scores - fresh[..., None])
        mass = mass * shrink + jnp.sum(probs, axis=-1)
        update = jnp.einsum(
            "qkgs,skd->qkgd",
            probs.astype(jnp.bfloat16),
            value_view,
            preferred_element_type=jnp.float32,
        )
        summed = summed * shrink[..., None] + update
        return (fresh, mass, summed)

    def unchanged(state):
        return state

    return lax.cond(useful, compute, unchanged, carry)


def fold_keys(carry, pieces, context):
    keys, values = pieces
    width = keys.shape[0]
    size = min(width, 1024)
    whole = width // size

    def one_block(index, state):
        offset = (index * size).astype(jnp.int32)
        key_part = lax.dynamic_slice_in_dim(keys, offset, size, 0)
        value_part = lax.dynamic_slice_in_dim(values, offset, size, 0)
        return attend_block(state, key_part, value_part, offset, context)

    carry = lax.fori_loop(0, whole, one_block, carry)
    return carry


def body(tokens, norm_gain, w_query, key_weight, value_weight, w_out, lengths):
    gathered = lax.all_gather(tokens, "tensor", axis=0, tiled=True)
    count = gathered.shape[0]
    first = lax.axis_index("dp") * count
    positions = first + jnp.arange(count, dtype=jnp.int32)
    starts = doc_starts(lengths, positions)
    query_rows, key, value_rows = project(
        gathered, norm_gain, w_query, key_weight, value_weight, positions, starts
    )
    heads = key.shape[1] // HEAD_SIZE
    query_rows = query_rows.reshape(count, heads, -1, HEAD_SIZE)
    group_count = query_rows.shape[2]
    context = (query_rows, positions, starts)
    initial = (
        jnp.full((count, heads, group_count), initial_peak, jnp.float32),
        jnp.zeros((count, heads, group_count), jnp.float32),
        jnp.zeros((count, heads, group_count, HEAD_SIZE), jnp.float32),
    )
    carry = fold_keys(initial, in_one_piece((key, value_rows), "dp", 0, 1), context)
    peak, mass, summed = carry
    attended = (summed / mass[..., None]).reshape(count, -1).astype(jnp.bfloat16)
    branch = lax.psum_scatter(
        jnp.dot(attended, w_out, preferred_element_type=jnp.float32).astype(jnp.bfloat16),
        "tensor",
        scatter_dimension=0,
        tiled=True,
    ).astype(jnp.float32)
    return (tokens.astype(jnp.float32) + branch).astype(jnp.bfloat16)


def solution(mesh):
    in_specs = (
        P(("dp", "tensor"), None),
        P(),
        P(None, "tensor"),
        P(None, "tensor"),
        P(None, "tensor"),
        P("tensor", None),
        P(),
    )
    out_specs = P(("dp", "tensor"), None)
    return jax.shard_map(body, mesh=mesh, in_specs=in_specs, out_specs=out_specs, check_vma=False)
```

profile of v0, /device:TPU:1, one launch (start us, length us, event | category | flops | bytes accessed | tf_op | source)
XLA Modules:
  0.0 329.1 jit_solution(13975362636619700645)
XLA Ops:
  6.5 0.7 all-gather.3.cloned.1.call-update
  7.3 0.7 copy.19
  8.2 0.7 select_reduce_fusion
  9.0 51.3 %all-gather.3.cloned.1.call-done = bf16[512,4096]{1,0:T(8,128)(2,1)} async-done(((bf16[128,4096]{1,0:T(8,128)(2,1)}), bf16[512,4096]{1,0:T(8,128)(2,1)}) %all-gather.3.cloned.1.call-update) | async-done | bytes 4194320 | tf_op jit(solution)/shard_map/all_gather | solution.py:117
  60.3 3.2 fusion.24
  63.7 1.6 convolution_bitcast_fusion
  65.9 1.6 convolution_convert_fusion.1
  67.5 0.7 pad_maximum_fusion.1
  68.5 1.8 multiply_cosine_fusion
  70.3 5.9 %fusion.39 = f32[512,512]{0,1:T(8,128)S(1)} fusion(bf16[4096,512]{1,0:T(8,128)(2,1)} %param.13, bf16[512,4096]{1,0:T(8,128)(2,1)} %all-gather.3.cloned.1.call-done, f32[4096]{0:T(1024)S(1)} %copy-done.4, f32[512]{0:T(512)S(1)} %add_rsqrt_fusion), kind=kOutput, calls=%fused_computation.61 | convolution fusion | flops 2155872256 | bytes 9455616 | tf_op jit(solution)/shard_map/dot_general | solution.py:49
  76.2 0.9 fusion.44
  77.5 1.4 copy.24
  78.9 1.2 fusion.27
  80.4 47.9 %all-gather.5.cloned.1.call-done = bf16[16384,256]{0,1:T(8,128)(2,1)} async-done(((bf16[512,256]{0,1:T(8,128)(2,1)}), bf16[16384,256]{0,1:T(8,128)(2,1)}) %all-gather.5.cloned.1.call-update) | async-done | bytes 8388624 | tf_op jit(solution)/shard_map/all_gather | solution.py:19
  128.3 5.8 %fusion.43 = (bf16[16384,128]{0,1:T(8,128)(2,1)}, bf16[16384,128]{0,1:T(8,128)(2,1)}) fusion(bf16[16384,256]{0,1:T(8,128)(2,1)} %all-gather.5.cloned.1.call-done), kind=kLoop, calls=%fused_computation.62 | loop fusion | bytes 16777216 | tf_op jit(solution)/shard_map/split | solution.py:19
  134.0 6.4 %copy.22 = bf16[16384,128]{1,0:T(8,128)(2,1)} copy(bf16[16384,128]{0,1:T(8,128)(2,1)} %get-tuple-element.495) | data formatting | bytes 8388608 | tf_op jit(solution)/shard_map/while | solution.py:112
  140.5 51.2 %while.21 = (s32[]{:T(128)}, f32[512,1,4]{0,2,1:T(4,128)S(1)}, f32[512,1,4]{0,2,1:T(4,128)S(1)}, f32[512,1,4,128]{0,3,2,1:T(8,128)S(1)}, s32[512]{0:T(512)S(1)},...) while((s32[]{:T(128)}, f32[512,1,4]{0,2,1:T(4,128)S(1)}, ...), condition=%wide.region_8.9_spmd, body=%wide.region_3.8_spmd.sunk | while | flops 1098914816 | bytes 30560620 | solution.py:112
  141.8 0.6 slice.63
  143.2 8.5 %conditional.2 = ((f32[512,1,4]{0,2,1:T(4,128)S(1)}, f32[512,1,4]{0,2,1:T(4,128)S(1)}, f32[512,1,4,128]{0,3,2,1:T(8,128)S(1)})) conditional(s32[]{:T(128)} %convert_element_type.108, (f32[512,1,4]{0,2,1:T(4,128)S(1)}, f32[512,1,4]{0,2,1:T(4,128)S(1)}, f32[512,1,4,128]{0,3,2,1:T(8,128)S(1)}) %tuple.77, (s32[]{:T(128)}, s32[1024]{0:T(1024)S(1)}, ...), branch_computations={%region_4.4_spmd, %region_5.7_spmd} | conditional | flops 1098914816 | bytes 30556238 | solution.py:97
  143.7 2.5 fusion.2
  146.2 3.5 %fusion.10 = f32[512,1,4,128]{0,3,2,1:T(8,128)S(1)} fusion(f32[1024,512,4]{1,0,2:T(8,128)S(1)} %get-tuple-element.493, f32[512,4]{0,1:T(4,128)S(1)} %bitcast.76, pred[512,1024]{0,1:T(8,128)(4,1)S(1)} %compare_and_fusion, f32[512,1,4,128]{0,3,2,1:T(8,128)S(1)} %get-tuple-element.426, f32[512,4]{0,1:T(4,128)S(1)} %get-tuple-element.490, ...), kind=kOutput, calls=%fused_computation.10 | convolution fusion | flops 545783808 | bytes 11288580 | tf_op jit(solution)/shard_map/while/body/eval_jaxpr/cond/branch_1_fun/qkgs,skd->qkgd/dot_general | solution.py:85
  149.8 1.8 fusion.1
  152.9 0.6 slice.63
  155.6 0.6 slice.63
  160.9 0.6 slice.63
  163.5 0.6 slice.63
  166.2 0.6 slice.63
  168.9 0.6 slice.63
  174.2 0.6 slice.63
  191.8 6.5 %convolution_convert_fusion = bf16[512,4096]{1,0:T(8,128)(2,1)} fusion(bf16[512,512]{0,1:T(8,128)(2,1)S(1)} %bitcast.78, bf16[512,4096]{1,0:T(8,128)(2,1)} %param.16), kind=kOutput, calls=%fused_computation.31 | convolution fusion | flops 2149580800 | bytes 8912896 | tf_op jit(solution)/shard_map/dot_general | solution.py:138
  198.4 121.8 %reduce-scatter.2.cloned.1.call-done = bf16[128,4096]{1,0:T(8,128)(2,1)} async-done(((bf16[512,4096]{1,0:T(8,128)(2,1)}), bf16[128,4096]{1,0:T(8,128)(2,1)}) %reduce-scatter.2.cloned.1.call-update) | async-done | bytes 1048592 | tf_op jit(solution)/shard_map/reduce_scatter | solution.py:137
  320.1 2.4 add_convert_fusion
  (88 shorter events, 17.3 us)
Async XLA Ops:
  6.5 57.0 %copy-start = (bf16[4096,128]{1,0:T(8,128)(2,1)S(1)}, bf16[4096,128]{1,0:T(8,128)(2,1)}, u32[]{:S(2)}) copy-start(bf16[4096,128]{1,0:T(8,128)(2,1)} %param.14) | copy-start | bytes 3145732
  6.5 57.0 %copy-start.4 = (f32[4096]{0:T(1024)S(1)}, f32[4096]{0:T(1024)}, u32[]{:S(2)}) copy-start(f32[4096]{0:T(1024)} %param.12) | copy-start | bytes 49156
  6.5 53.7 %all-gather.3.cloned.1.call-start = ((), (), s32[]{:S(2)}) async-start(), calls=%async_computation.1 | async-start | bytes 5242880 | tf_op jit(solution)/shard_map/all_gather | solution.py:117
  7.3 121.0 %all-gather.5.cloned.1.call-start = ((), (), s32[]{:S(2)}) async-start(), calls=%async_computation.2 | async-start | bytes 8650752 | tf_op jit(solution)/shard_map/all_gather | solution.py:19
  60.3 3.4 %copy-start.2 = (bf16[512,4096]{1,0:T(8,128)(2,1)S(1)}, bf16[512,4096]{1,0:T(8,128)(2,1)}, u32[]{:S(2)}) copy-start(bf16[512,4096]{1,0:T(8,128)(2,1)} %all-gather.3.cloned.1.call-done) | copy-start | bytes 12582916
  63.7 2.2 copy-start.3
  68.3 251.8 %reduce-scatter.2.cloned.1.call-start = ((), (), s32[]{:S(2)}) async-start(), calls=%async_computation.3 | async-start | bytes 5242880 | tf_op jit(solution)/shard_map/reduce_scatter | solution.py:137
  198.3 121.8 %copy-start.1 = (bf16[128,4096]{1,0:T(8,128)(2,1)S(1)}, bf16[128,4096]{1,0:T(8,128)(2,1)}, u32[]{:S(2)}) copy-start(bf16[128,4096]{1,0:T(8,128)(2,1)} %param.11) | copy-start | bytes 3145732
Sparse Core Ops, SparseCore 0:
  9.0 51.2 all-gather.2
  68.4 59.7 all-gather.4
  198.5 121.6 reduce-scatter.1
where the time goes:
time: 330 us; the launch traced here: 329 us
  waiting for transfers between devices  222 us (67%)
  local copies, waits for them, and re-layouts  35.5 us (11%)
  loops' own time  23.1 us (7%)
  matrix products  21.7 us (7%)
  other arithmetic  13.7 us (4%)
  between operations  13.2 us (4%)
    reduce_scatter x1, waiting for transfers between devices, body(): lax.psum_scatter(jnp.dot(attended, w_out, preferred_element_type=jnp.floa...  122 us
    all_gather x1, waiting for transfers between devices, body(): gathered = lax.all_gather(tokens, 'tensor', axis=0, tiled=True)  51.3 us
    all_gather x1, waiting for transfers between devices, in_one_piece(): lax.all_gather(both, axis, axis=dim, tiled=True)  47.9 us
    another operation x1, loops' own time, fold_keys(): carry = lax.fori_loop(0, whole, one_block, carry)  22.8 us
    slice x16, local copies, waits for them, and re-layouts, attend_block(): positions[-1]  10.4 us
    slice x16, local copies, waits for them, and re-layouts, attend_block(): starts[0]  9.25 us
  transfers between devices with their start and end apart: 3, of which 3 were waited for; matrix products, arithmetic and copies ran while one was open for 4% of the time, Pallas kernels for 0%

commit v1 on v0

--- a/solution.py
+++ b/solution.py
@@ -114,7 +114,9 @@
 
 
 def body(tokens, norm_gain, w_query, key_weight, value_weight, w_out, lengths):
-    gathered = lax.all_gather(tokens, "tensor", axis=0, tiled=True)
+    gathered = jnp.concatenate(
+        lax.all_to_all(jnp.stack([tokens] * lax.axis_size("tensor")), "tensor", 0, 0), axis=0
+    )
     count = gathered.shape[0]
     first = lax.axis_index("dp") * count
     positions = first + jnp.arange(count, dtype=jnp.int32)

time: 330 us -> 336 us (1.018)
  local copies, waits for them, and re-layouts: 35.5 us -> 41.4 us
  starting transfers between devices: 0.26 us -> 5.36 us
  waiting for transfers between devices: 222 us -> 217 us
  other arithmetic: 13.7 us -> 18.1 us
  matrix products: 21.7 us -> 18.1 us
    all_gather x1 -> x0, waiting for transfers between devices: 51.3 us -> none  [body(): gathered = lax.all_gather(tokens, 'tensor', axis=0, tiled=True)]
    all_to_all x0 -> x1, waiting for transfers between devices: none -> 48.5 us  [body(): lax.all_to_all(jnp.stack([tokens] * lax.axis_size('tensor')), 'tensor', 0...]
    convert_element_type x0 -> x2, other arithmetic: none -> 7.8 us  [project(): normed = (wide * inverse * norm_gain[None, :]).astype(jnp.bfloat16)]
    dot_general x0 -> x1, local copies, waits for them, and re-layouts: none -> 6.41 us  [project(): jnp.dot(normed, w_query, preferred_element_type=jnp.float32)]
    all_to_all x0 -> x1, starting transfers between devices: none -> 5.13 us  [body(): lax.all_to_all(jnp.stack([tokens] * lax.axis_size('tensor')), 'tensor', 0...]
    dot_general x1, matrix products: 5.92 us -> 2.36 us  [project(): jnp.dot(normed, w_query, preferred_element_type=jnp.float32)]
where the time goes in v1:
time: 336 us; the launch traced here: 334 us
  waiting for transfers between devices  217 us (65%)
  local copies, waits for them, and re-layouts  41.4 us (12%)
  loops' own time  20.8 us (6%)
  other arithmetic  18.1 us (5%)
  matrix products  18.1 us (5%)
  between operations  13.6 us (4%)
  starting transfers between devices  5.36 us (2%)
    reduce_scatter x1, waiting for transfers between devices, body(): lax.psum_scatter(jnp.dot(attended, w_out, preferred_element_type=jnp.floa...  122 us
    all_to_all x1, waiting for transfers between devices, body(): lax.all_to_all(jnp.stack([tokens] * lax.axis_size('tensor')), 'tensor', 0...  48.5 us
    all_gather x1, waiting for transfers between devices, in_one_piece(): lax.all_gather(both, axis, axis=dim, tiled=True)  46.8 us
    another operation x1, loops' own time, fold_keys(): carry = lax.fori_loop(0, whole, one_block, carry)  20.5 us
    slice x16, local copies, waits for them, and re-layouts, attend_block(): positions[-1]  9.8 us
    slice x16, local copies, waits for them, and re-layouts, attend_block(): starts[0]  8.68 us
    convert_element_type x2, other arithmetic, project(): normed = (wide * inverse * norm_gain[None, :]).astype(jnp.bfloat16)  7.8 us
  transfers between devices with their start and end apart: 3, of which 3 were waited for; matrix products, arithmetic and copies ran while one was open for 4% of the time, Pallas kernels for 0%

profile of v1, /device:TPU:1, one launch (start us, length us, event | category | flops | bytes accessed | tf_op | source)
XLA Modules:
  0.0 334.4 jit_solution(15973999207493445657)
XLA Ops:
  6.5 3.8 %stack.2 = bf16[4,128,4096]{2,1,0:T(8,128)(2,1)} broadcast(bf16[128,4096]{1,0:T(8,128)(2,1)} %param.11), dimensions={1,2} | broadcast | bytes 5242880 | tf_op jit(solution)/shard_map/stack | solution.py:118
  10.3 5.1 %all-to-all-start = ((bf16[4,128,4096]{2,1,0:T(8,128)(2,1)}), bf16[4,128,4096]{2,1,0:T(8,128)(2,1)}, u32[]{:S(2)}, u32[]{:S(2)}) async-start(bf16[4,128,4096]{2,1,0:T(8,128)(2,1)} %stack.2), calls=%async_computation | async-start | bytes 8388608 | tf_op jit(solution)/shard_map/all_to_all | solution.py:118
  15.8 48.5 %all-to-all-done = bf16[4,128,4096]{2,1,0:T(8,128)(2,1)} async-done(((bf16[4,128,4096]{2,1,0:T(8,128)(2,1)}), bf16[4,128,4096]{2,1,0:T(8,128)(2,1)}, u32[]{:S(2)}, u32[]{:S(2)}) %all-to-all-start) | async-done | bytes 4194336 | tf_op jit(solution)/shard_map/all_to_all | solution.py:118
  64.3 3.1 multiply_reduce_fusion
  67.4 3.8 %fusion.25 = bf16[512,4096]{1,0:T(8,128)(2,1)S(1)} fusion(bf16[4,128,4096]{2,1,0:T(8,128)(2,1)} %all-to-all-done, f32[4096]{0:T(1024)S(1)} %copy-done.5, f32[512]{0:T(512)S(1)} %get-tuple-element.503), kind=kLoop, calls=%fused_computation.28 | loop fusion | flops 8388608 | bytes 8407040 | tf_op jit(solution)/shard_map/convert_element_type | solution.py:47
  71.3 1.5 convolution_convert_fusion.1
  72.8 1.5 convolution_bitcast_fusion
  74.9 0.7 pad_maximum_fusion.1
  75.9 6.4 %copy.24 = bf16[512,4096]{1,0:T(8,128)(2,1)} copy(bf16[512,4096]{0,1:T(8,128)(2,1)} %bitcast.92) | data formatting | bytes 8388608 | tf_op jit(solution)/shard_map/dot_general | solution.py:49
  82.9 4.0 %multiply_convert_fusion = bf16[4,128,4096]{2,1,0:T(8,128)(2,1)S(1)} fusion(bf16[4,128,4096]{2,1,0:T(8,128)(2,1)} %all-to-all-done, f32[4096]{0:T(1024)S(1)} %copy-done.5, f32[4,128]{1,0:T(4,128)S(1)} %get-tuple-element.502), kind=kLoop, calls=%fused_computation.29 | loop fusion | flops 8388608 | bytes 8407040 | tf_op jit(solution)/shard_map/convert_element_type | solution.py:47
  86.9 2.4 fusion.40
  89.7 46.8 %all-gather.2.cloned.1.call-done = bf16[16384,256]{0,1:T(8,128)(2,1)} async-done(((bf16[512,256]{0,1:T(8,128)(2,1)}), bf16[16384,256]{0,1:T(8,128)(2,1)}) %all-gather.2.cloned.1.call-update) | async-done | bytes 8388624 | tf_op jit(solution)/shard_map/all_gather | solution.py:19
  136.5 5.8 %fusion.39 = (bf16[16384,128]{0,1:T(8,128)(2,1)}, bf16[16384,128]{0,1:T(8,128)(2,1)}) fusion(bf16[16384,256]{0,1:T(8,128)(2,1)} %all-gather.2.cloned.1.call-done), kind=kLoop, calls=%fused_computation.62 | loop fusion | bytes 16777216 | tf_op jit(solution)/shard_map/split | solution.py:19
  142.3 6.4 %copy.21 = bf16[16384,128]{1,0:T(8,128)(2,1)} copy(bf16[16384,128]{0,1:T(8,128)(2,1)} %get-tuple-element.495) | data formatting | bytes 8388608 | tf_op jit(solution)/shard_map/while | solution.py:112
  148.8 47.7 %while.21 = (s32[]{:T(128)}, f32[512,1,4]{0,2,1:T(4,128)S(1)}, f32[512,1,4]{0,2,1:T(4,128)S(1)}, f32[512,1,4,128]{0,3,2,1:T(8,128)S(1)}, s32[512]{0:T(512)S(1)},...) while((s32[]{:T(128)}, f32[512,1,4]{0,2,1:T(4,128)S(1)}, ...), condition=%wide.region_8.9_spmd, body=%wide.region_3.8_spmd.sunk | while | flops 1098914816 | bytes 30560620 | solution.py:112
  151.2 8.5 %conditional.2 = ((f32[512,1,4]{0,2,1:T(4,128)S(1)}, f32[512,1,4]{0,2,1:T(4,128)S(1)}, f32[512,1,4,128]{0,3,2,1:T(8,128)S(1)})) conditional(s32[]{:T(128)} %convert_element_type.115, (f32[512,1,4]{0,2,1:T(4,128)S(1)}, f32[512,1,4]{0,2,1:T(4,128)S(1)}, f32[512,1,4,128]{0,3,2,1:T(8,128)S(1)}) %tuple.77, (s32[]{:T(128)}, s32[1024]{0:T(1024)S(1)}, ...), branch_computations={%region_4.4_spmd, %region_5.7_spmd} | conditional | flops 1098914816 | bytes 30556238 | solution.py:97
  151.7 2.5 fusion.2
  154.3 3.5 %fusion.10 = f32[512,1,4,128]{0,3,2,1:T(8,128)S(1)} fusion(f32[1024,512,4]{1,0,2:T(8,128)S(1)} %get-tuple-element.493, f32[512,4]{0,1:T(4,128)S(1)} %bitcast.94, pred[512,1024]{0,1:T(8,128)(4,1)S(1)} %compare_and_fusion, f32[512,1,4,128]{0,3,2,1:T(8,128)S(1)} %get-tuple-element.426, f32[512,4]{0,1:T(4,128)S(1)} %get-tuple-element.490, ...), kind=kOutput, calls=%fused_computation.10 | convolution fusion | flops 545783808 | bytes 11288580 | tf_op jit(solution)/shard_map/while/body/eval_jaxpr/cond/branch_1_fun/qkgs,skd->qkgd/dot_general | solution.py:85
  157.8 1.8 fusion.1
  160.9 0.6 slice.73
  163.3 0.6 slice.73
  165.7 0.6 slice.73
  168.2 0.6 slice.73
  170.6 0.6 slice.73
  173.1 0.6 slice.73
  175.5 0.6 slice.73
  177.9 0.6 slice.73
  180.4 0.6 slice.73
  182.8 0.6 slice.73
  196.7 6.6 %convolution_convert_fusion = bf16[512,4096]{1,0:T(8,128)(2,1)} fusion(bf16[512,512]{0,1:T(8,128)(2,1)S(1)} %bitcast.96, bf16[512,4096]{1,0:T(8,128)(2,1)} %param.16), kind=kOutput, calls=%fused_computation.31 | convolution fusion | flops 2149580800 | bytes 8912896 | tf_op jit(solution)/shard_map/dot_general | solution.py:140
  203.3 121.8 %reduce-scatter.2.cloned.1.call-done = bf16[128,4096]{1,0:T(8,128)(2,1)} async-done(((bf16[512,4096]{1,0:T(8,128)(2,1)}), bf16[128,4096]{1,0:T(8,128)(2,1)}) %reduce-scatter.2.cloned.1.call-update) | async-done | bytes 1048592 | tf_op jit(solution)/shard_map/reduce_scatter | solution.py:139
  325.1 2.4 add_convert_fusion
  (93 shorter events, 15.6 us)
Async XLA Ops:
  6.5 64.7 %copy-start = (bf16[4096,128]{1,0:T(8,128)(2,1)S(1)}, bf16[4096,128]{1,0:T(8,128)(2,1)}, u32[]{:S(2)}) copy-start(bf16[4096,128]{1,0:T(8,128)(2,1)} %param.15) | copy-start | bytes 3145732
  10.3 5.1 %copy-start.6 = (s32[16]{0:T(128)S(1)}, s32[16]{0:T(128)}, u32[]{:S(2)}) copy-start(s32[16]{0:T(128)} %param.17) | copy-start | bytes 196
  10.3 54.0 %all-to-all-start = ((bf16[4,128,4096]{2,1,0:T(8,128)(2,1)}), bf16[4,128,4096]{2,1,0:T(8,128)(2,1)}, u32[]{:S(2)}, u32[]{:S(2)}) async-start(bf16[4,128,4096]{2,1,0:T(8,128)(2,1)} %stack.2), calls=%async_computation | async-start | bytes 8388608 | tf_op jit(solution)/shard_map/all_to_all | solution.py:118
  15.4 52.0 %copy-start.5 = (f32[4096]{0:T(1024)S(1)}, f32[4096]{0:T(1024)}, u32[]{:S(2)}) copy-start(f32[4096]{0:T(1024)} %param.12) | copy-start | bytes 49156
  15.4 121.1 %all-gather.2.cloned.1.call-start = ((), (), s32[]{:S(2)}) async-start(), calls=%async_computation.2 | async-start | bytes 8650752 | tf_op jit(solution)/shard_map/all_gather | solution.py:19
  71.3 1.6 copy-start.4
  75.7 249.4 %reduce-scatter.2.cloned.1.call-start = ((), (), s32[]{:S(2)}) async-start(), calls=%async_computation.3 | async-start | bytes 5242880 | tf_op jit(solution)/shard_map/reduce_scatter | solution.py:139
  82.9 4.0 %copy-start.3 = (bf16[512,4096]{1,0:T(8,128)(2,1)S(1)}, bf16[512,4096]{1,0:T(8,128)(2,1)}, u32[]{:S(2)}) copy-start(bf16[512,4096]{1,0:T(8,128)(2,1)} %copy.24) | copy-start | bytes 12582916
  196.7 130.9 %copy-start.1 = (bf16[4096,128]{1,0:T(8,128)(2,1)S(1)}, bf16[4096,128]{1,0:T(8,128)(2,1)}, u32[]{:S(2)}) copy-start(bf16[4096,128]{1,0:T(8,128)(2,1)} %param.15) | copy-start | bytes 3145732
  203.3 121.8 %copy-start.2 = (bf16[128,4096]{1,0:T(8,128)(2,1)S(1)}, bf16[128,4096]{1,0:T(8,128)(2,1)}, u32[]{:S(2)}) copy-start(bf16[128,4096]{1,0:T(8,128)(2,1)} %param.11) | copy-start | bytes 3145732
Sparse Core Ops, SparseCore 0:
  75.8 60.6 all-gather.1
  203.4 121.6 reduce-scatter.1
